TPU v7x, 32 devices: a whole 2x2x4 slice. The times are simulated.
32 devices in a mesh: dp: 16 (over z, x, core), gene: 2 (over y).
Axes of the slice: x: 2, y: 2, z: 4, core: 2. Of those that a mesh axis runs over, the one named last changes fastest.
Arguments:
- counts: int32 [4096, 13500], P('dp', 'gene'), may hold values from 0 to 15, as said below
- coords: float32 [4096, 2], P(('dp', 'gene')), may hold values from 0 to 100
- segments: int32 [32, 128], P(('dp', 'gene')), may hold values from 0 to 3, never falling along the last dimension, each value on 1 to 64 neighbouring positions
- noise: float32 [4096, 512], P(('dp', 'gene')), may hold values from -6 to 6
- embed_table: bfloat16 [13500, 1024], P('gene'), may hold values from -0.0546875 to 0.0546875
- ln1_gain: float32 [1024], replicated, may hold values from 0.5 to 1.5
- ln1_bias: float32 [1024], replicated, may hold values from -1 to 1
- w_qkv: bfloat16 [1024, 3072], replicated, may hold values from -0.1875 to 0.1875
- w_out: bfloat16 [1024, 1024], replicated, may hold values from -0.375 to 0.375
- ln2_gain: float32 [1024], replicated, may hold values from 0.5 to 1.5
- ln2_bias: float32 [1024], replicated, may hold values from -1 to 1
- w_up: bfloat16 [1024, 4096], replicated, may hold values from -0.1875 to 0.1875
- w_down: bfloat16 [4096, 1024], replicated, may hold values from -0.09375 to 0.09375
- w_latent: bfloat16 [1024, 1024], replicated, may hold values from -0.09375 to 0.09375
- mix_means: float32 [16, 512], replicated, may hold values from -0.4 to 0.4
- mix_logits: float32 [16], replicated, may hold values from -4 to 4
- w_decode: bfloat16 [512, 13500], P(None, 'gene'), may hold values from -0.25 to 0.25
Outputs:
- block_out: bfloat16 [4096, 1024], P(('dp', 'gene'))
- loss: float32 [], replicated
- grad_input: float32 [4096, 1024], P(('dp', 'gene'))
- grad_table: float32 [1024, 13500], P('dp', 'gene')
- grad_decode: float32 [512, 13500], P('dp', 'gene')
- grad_qkv: float32 [1024, 3072], P('dp', 'gene')
- grad_out: float32 [1024, 1024], P('dp', 'gene')
- grad_ln1_gain: float32 [1024], replicated
- grad_ln1_bias: float32 [1024], replicated
- grad_ln2_gain: float32 [1024], replicated
- grad_ln2_bias: float32 [1024], replicated
- grad_up: float32 [1024, 4096], P('dp', 'gene')
- grad_down: float32 [4096, 1024], P('dp', 'gene')
- grad_latent: float32 [1024, 1024], P('dp', 'gene')
- grad_means: float32 [16, 512], replicated
- grad_logits: float32 [16], replicated
Inputs may be any that keep to these rules, and one draw needn't show every extreme that they name: `counts`: about a quarter of the entries are nonzero. `segments`: along each row the ids never fall; each of the 4 slides of a row holds 1 to 64 cells, one exactly 64.
All inputs are finite; a program needn't handle non-finite values.
Results may differ from a plain program's by a relative error of at most 0.013.
Values may be sent and summed in bfloat16 or wider, within the bound.
A program may use at most 384 MiB of HBM per device.

v0:
```python
import math

import jax
import jax.numpy as jnp
from jax import lax
from jax.sharding import PartitionSpec as P

D = 1024
HEADS = 16
HDIM = 64
LAT = 512
G = 13500


ln_eps = 1e-05
root_half = 0.7071067811865476
inv_root_two_pi = 0.3989422804014327
mask_floor = -1e30


def product(left, right):
    return jnp.dot(left, right, preferred_element_type=jnp.float32)


def product_left(left, right):
    return lax.dot_general(
        left, right, (((0,), (0,)), ((), ())), preferred_element_type=jnp.float32
    )


def product_right(left, right):
    return lax.dot_general(
        left, right, (((1,), (1,)), ((), ())), preferred_element_type=jnp.float32
    )


def precise(left, right):
    return jnp.dot(left, right, precision=lax.Precision.HIGHEST, preferred_element_type=jnp.float32)


def position_code(coords):
    quarter = D // 4
    freq = jnp.exp(-jnp.arange(quarter, dtype=jnp.float32) * (math.log(100.0) / quarter))
    along_x = coords[:, 0:1] * freq[None, :]
    along_y = coords[:, 1:2] * freq[None, :]
    return jnp.concatenate(
        [jnp.sin(along_x), jnp.cos(along_x), jnp.sin(along_y), jnp.cos(along_y)], axis=1
    )


def norm_forward(values, gain, bias):
    center = values - jnp.mean(values, axis=-1, keepdims=True)
    spread = lax.rsqrt(jnp.mean(center * center, axis=-1, keepdims=True) + ln_eps)
    normal = center * spread
    return (normal * gain + bias, normal, spread)


def norm_backward(grad_out, normal, spread, gain):
    grad_normal = grad_out * gain
    inner = (
        grad_normal
        - jnp.mean(grad_normal, axis=-1, keepdims=True)
        - normal * jnp.mean(grad_normal * normal, axis=-1, keepdims=True)
    )
    return (spread * inner, jnp.sum(grad_out * normal, axis=0), jnp.sum(grad_out, axis=0))


def shards(
    counts,
    coords,
    segments,
    noise,
    embed_table,
    ln1_gain,
    ln1_bias,
    w_qkv,
    w_out,
    ln2_gain,
    ln2_bias,
    w_up,
    w_down,
    w_latent,
    mix_means,
    mix_logits,
    w_decode,
):
    cells = coords.shape[0]
    all_cells = cells * lax.axis_size("dp") * lax.axis_size("gene")
    factor = 1.0 / (all_cells * G)
    scale = HDIM ** (-0.5)
    target = jnp.log1p(counts.astype(jnp.float32))
    expr_low = target.astype(jnp.bfloat16)
    embedded = lax.psum_scatter(
        product(expr_low, embed_table), "gene", scatter_dimension=0, tiled=True
    )
    state_in = embedded + position_code(coords)
    normed1, unit1, spread1 = norm_forward(state_in, ln1_gain, ln1_bias)
    normed1 = normed1.astype(jnp.bfloat16)
    qkv_low = product(normed1, w_qkv).astype(jnp.bfloat16)
    query = qkv_low[:, :D].reshape(cells, HEADS, HDIM)
    keys = qkv_low[:, D : 2 * D].reshape(cells, HEADS, HDIM)
    values = qkv_low[:, 2 * D :].reshape(cells, HEADS, HDIM)
    slide = segments[0]
    same = (slide[:, None] == slide[None, :])[None]
    scores = jnp.einsum("qhd,khd->hqk", query, keys, preferred_element_type=jnp.float32) * scale
    scores = jnp.where(same, scores, mask_floor)
    peak = jnp.max(scores, axis=-1, keepdims=True)
    expo = jnp.exp(scores - peak)
    probs = expo / jnp.sum(expo, axis=-1, keepdims=True)
    probs_low = probs.astype(jnp.bfloat16)
    attended = jnp.einsum("hqk,khd->qhd", probs_low, values, preferred_element_type=jnp.float32)
    attended = attended.reshape(cells, D).astype(jnp.bfloat16)
    state_mid = state_in + product(attended, w_out)
    normed2, unit2, spread2 = norm_forward(state_mid, ln2_gain, ln2_bias)
    normed2 = normed2.astype(jnp.bfloat16)
    pre_act = product(normed2, w_up)
    cumul = 0.5 * (1.0 + lax.erf(pre_act * root_half))
    active = (pre_act * cumul).astype(jnp.bfloat16)
    state_out = state_mid + product(active, w_down)
    out_low = state_out.astype(jnp.bfloat16)
    latent = product(out_low, w_latent)
    center = latent[:, :LAT]
    log_var = latent[:, LAT:]
    deviation = jnp.exp(0.5 * log_var)
    sample = center + deviation * noise
    sample_low = sample.astype(jnp.bfloat16)
    sample_all = lax.all_gather(sample_low, "gene", axis=0, tiled=True)
    predicted = product(sample_all, w_decode)
    error = predicted - target
    recon = 0.5 * jnp.sum(error * error)
    grad_pred = (factor * error).astype(jnp.bfloat16)
    grad_dec_local = product_left(sample_all, grad_pred)
    grad_sample = lax.psum_scatter(
        product_right(grad_pred, w_decode), "gene", scatter_dimension=0, tiled=True
    )
    log_weight = jax.nn.log_softmax(mix_logits)
    dist = (
        jnp.sum(sample * sample, axis=1, keepdims=True)
        - 2.0 * precise(sample, mix_means.T)
        + jnp.sum(mix_means * mix_means, axis=1)[None, :]
    )
    mix_score = log_weight[None, :] - 0.5 * dist
    top = jnp.max(mix_score, axis=1, keepdims=True)
    shifted = jnp.exp(mix_score - top)
    totals = jnp.sum(shifted, axis=1, keepdims=True)
    share = shifted / totals
    mixture = jnp.sum(-0.5 * log_var) - jnp.sum(top + jnp.log(totals))
    loss_part = factor * (recon + mixture)
    grad_sample = grad_sample + factor * (sample - precise(share, mix_means))
    share_sum = jnp.sum(share, axis=0)
    grad_means_local = factor * (share_sum[:, None] * mix_means - precise(share.T, sample))
    weight_sum = -factor * share_sum
    grad_logits_local = weight_sum - jnp.exp(log_weight) * jnp.sum(weight_sum)
    grad_logvar = -0.5 * factor + grad_sample * 0.5 * deviation * noise
    grad_lat_low = jnp.concatenate([grad_sample, grad_logvar], axis=1).astype(jnp.bfloat16)
    grad_w_latent = product_left(out_low, grad_lat_low)
    grad_state = product_right(grad_lat_low, w_latent)
    grad_branch = grad_state.astype(jnp.bfloat16)
    grad_w_down = product_left(active, grad_branch)
    grad_active = product_right(grad_branch, w_down)
    slope = cumul + pre_act * jnp.exp(-0.5 * pre_act * pre_act) * inv_root_two_pi
    grad_pre = (grad_active * slope).astype(jnp.bfloat16)
    grad_w_up = product_left(normed2, grad_pre)
    grad_normed2 = product_right(grad_pre, w_up)
    back_two, grad_gain2, grad_bias2 = norm_backward(grad_normed2, unit2, spread2, ln2_gain)
    grad_state = grad_state + back_two
    grad_attn_low = grad_state.astype(jnp.bfloat16)
    grad_w_out = product_left(attended, grad_attn_low)
    grad_attended = (
        product_right(grad_attn_low, w_out).astype(jnp.bfloat16).reshape(cells, HEADS, HDIM)
    )
    grad_probs = jnp.einsum(
        "qhd,khd->hqk", grad_attended, values, preferred_element_type=jnp.float32
    )
    row_inner = jnp.sum(probs * grad_probs, axis=-1, keepdims=True)
    grad_scores = (probs * (grad_probs - row_inner)).astype(jnp.bfloat16)
    grad_query = (
        jnp.einsum("hqk,khd->qhd", grad_scores, keys, preferred_element_type=jnp.float32) * scale
    )
    grad_keys = (
        jnp.einsum("hqk,qhd->khd", grad_scores, query, preferred_element_type=jnp.float32) * scale
    )
    grad_values = jnp.einsum(
        "hqk,qhd->khd", probs_low, grad_attended, preferred_element_type=jnp.float32
    )
    grad_qkv_low = jnp.concatenate(
        [grad_query.reshape(cells, D), grad_keys.reshape(cells, D), grad_values.reshape(cells, D)],
        axis=1,
    ).astype(jnp.bfloat16)
    grad_w_qkv = product_left(normed1, grad_qkv_low)
    grad_normed1 = product_right(grad_qkv_low, w_qkv)
    back_one, grad_gain1, grad_bias1 = norm_backward(grad_normed1, unit1, spread1, ln1_gain)
    grad_input = grad_state + back_one
    grad_embed_low = grad_input.astype(jnp.bfloat16)
    grad_table_local = product_left(
        lax.all_gather(grad_embed_low, "gene", axis=0, tiled=True), expr_low
    )
    table_part, decode_part = (
        lax.psum_scatter(grad_table_local, "dp", scatter_dimension=0, tiled=True),
        lax.psum_scatter(grad_dec_local, "dp", scatter_dimension=0, tiled=True),
    )
    gene_qkv, gene_out, gene_up, gene_down, gene_latent = (
        lax.psum_scatter(
            grad_w_qkv.astype(jnp.bfloat16), "gene", scatter_dimension=1, tiled=True
        ).astype(jnp.float32),
        lax.psum_scatter(
            grad_w_out.astype(jnp.bfloat16), "gene", scatter_dimension=1, tiled=True
        ).astype(jnp.float32),
        lax.psum_scatter(
            grad_w_up.astype(jnp.bfloat16), "gene", scatter_dimension=1, tiled=True
        ).astype(jnp.float32),
        lax.psum_scatter(
            grad_w_down.astype(jnp.bfloat16), "gene", scatter_dimension=1, tiled=True
        ).astype(jnp.float32),
        lax.psum_scatter(
            grad_w_latent.astype(jnp.bfloat16), "gene", scatter_dimension=1, tiled=True
        ).astype(jnp.float32),
    )
    sum_qkv, sum_out, sum_up, sum_down, sum_latent = (
        lax.psum_scatter(gene_qkv, "dp", scatter_dimension=0, tiled=True),
        lax.psum_scatter(gene_out, "dp", scatter_dimension=0, tiled=True),
        lax.psum_scatter(gene_up, "dp", scatter_dimension=0, tiled=True),
        lax.psum_scatter(gene_down, "dp", scatter_dimension=0, tiled=True),
        lax.psum_scatter(gene_latent, "dp", scatter_dimension=0, tiled=True),
    )
    loss_total, logits_total, means_total, sum_gain1, sum_bias1, sum_gain2, sum_bias2 = lax.psum(
        (
            loss_part,
            grad_logits_local,
            grad_means_local,
            grad_gain1,
            grad_bias1,
            grad_gain2,
            grad_bias2,
        ),
        ("dp", "gene"),
    )
    return (
        state_out.astype(jnp.bfloat16),
        loss_total,
        grad_input,
        table_part,
        decode_part,
        sum_qkv,
        sum_out,
        sum_gain1,
        sum_bias1,
        sum_gain2,
        sum_bias2,
        sum_up,
        sum_down,
        sum_latent,
        means_total,
        logits_total,
    )


def solution(mesh):
    in_specs = (
        P("dp", "gene"),
        P(("dp", "gene"), None),
        P(("dp", "gene"), None),
        P(("dp", "gene"), None),
        P("gene", None),
        P(),
        P(),
        P(),
        P(),
        P(),
        P(),
        P(),
        P(),
        P(),
        P(),
        P(),
        P(None, "gene"),
    )
    out_specs = (
        P(("dp", "gene"), None),
        P(),
        P(("dp", "gene"), None),
        P("dp", "gene"),
        P("dp", "gene"),
        P("dp", "gene"),
        P("dp", "gene"),
        P(),
        P(),
        P(),
        P(),
        P("dp", "gene"),
        P("dp", "gene"),
        P("dp", "gene"),
        P(),
        P(),
    )
    return jax.shard_map(shards, mesh=mesh, in_specs=in_specs, out_specs=out_specs, check_vma=False)
```

profile of v0, /device:TPU:0, one launch (start us, length us, event | category | flops | bytes accessed | tf_op | source)
XLA Modules:
  0.0 1327.2 jit_solution(6375517300653795864)
XLA Ops:
  7.3 12.3 fusion.12
  19.6 0.6 reduce-scatter.17.cloned.1.call-start
  20.3 1.0 multiply_sine_fusion.1
  21.3 21.6 %reduce-scatter.15.cloned.1.call-done = f32[128,1024]{1,0:T(8,128)} async-done(((f32[256,1024]{1,0:T(8,128)}), f32[128,1024]{1,0:T(8,128)}) %reduce-scatter.15.cloned.1.call-update) | async-done | bytes 524304 | tf_op jit(solution)/shard_map/reduce_scatter | solution.py:93
  42.9 1.2 fusion.50
  44.6 0.6 copy-done.56
  45.2 3.8 convolution_convert_fusion.3
  49.0 0.8 fusion.51
  50.0 1.2 copy.46
  51.2 0.8 copy.45
  52.0 1.5 fusion.52
  53.5 1.7 convolution_convert_fusion.8
  56.1 4.9 fusion.48
  61.1 5.6 fusion.16
  68.0 5.9 all_gather.6
  73.9 4.0 multiply_reduce_fusion
  77.8 2.8 copy-done.2
  80.7 2.8 fusion.15
  83.6 0.6 reduce_max.29
  84.2 1.2 exponential_reduce_fusion
  86.2 0.7 subtract_subtract_fusion
  87.8 10.5 reduce-scatter.17.cloned.1.call-done
  98.3 2.4 add_convert_fusion.2
  100.7 0.7 copy-done.16
  101.4 2.6 fusion.29
  104.0 6.6 fusion.2
  110.7 3.5 multiply_reduce_fusion.2
  114.5 0.8 copy-done.7
  115.3 2.0 convolution_convert_fusion.5
  117.6 3.0 convolution_convert_fusion.4
  120.7 2.6 convolution_convert_fusion.7
  123.3 1.3 copy.49
  124.6 2.5 convolution_convert_fusion.6
  129.5 4.7 convolution_convert_fusion.2
  134.3 1.5 copy-done.5
  135.8 5.6 convolution_convert_fusion
  141.5 1.1 copy-done.13
  142.7 5.7 convolution_convert_fusion.1
  148.4 1.0 reduce-scatter.27.cloned.1.call-done
  149.4 2.8 convert_element_type.112
  152.3 31.1 %reduce-scatter.39.cloned.1.call-done = bf16[1024,512]{1,0:T(8,128)(2,1)} async-done(((bf16[1024,1024]{1,0:T(8,128)(2,1)}), bf16[1024,512]{1,0:T(8,128)(2,1)}) %reduce-scatter.39.cloned.1.call-update) | async-done | bytes 1048592 | tf_op jit(solution)/shard_map/reduce_scatter | solution.py:215
  183.4 2.9 convert_element_type.118
  186.4 10.2 fusion.14
  196.6 66.1 %reduce-scatter.23.cloned.1.call-done = bf16[1024,1536]{1,0:T(8,128)(2,1)} async-done(((bf16[1024,3072]{1,0:T(8,128)(2,1)}), bf16[1024,1536]{1,0:T(8,128)(2,1)}) %reduce-scatter.23.cloned.1.call-update) | async-done | bytes 3145744 | tf_op jit(solution)/shard_map/reduce_scatter | solution.py:203
  262.7 5.5 convert_element_type.110
  268.5 95.7 %reduce-scatter.35.cloned.1.call-done = bf16[4096,512]{1,0:T(8,128)(2,1)} async-done(((bf16[4096,1024]{1,0:T(8,128)(2,1)}), bf16[4096,512]{1,0:T(8,128)(2,1)}) %reduce-scatter.35.cloned.1.call-update) | async-done | bytes 4194320 | tf_op jit(solution)/shard_map/reduce_scatter | solution.py:212
  364.2 6.6 convert_element_type.116
  370.9 95.0 %reduce-scatter.31.cloned.1.call-done = bf16[1024,2048]{1,0:T(8,128)(2,1)} async-done(((bf16[1024,4096]{1,0:T(8,128)(2,1)}), bf16[1024,2048]{1,0:T(8,128)(2,1)}) %reduce-scatter.31.cloned.1.call-update) | async-done | bytes 4194320 | tf_op jit(solution)/shard_map/reduce_scatter | solution.py:209
  465.9 6.4 convert_element_type.114
  472.4 0.9 copy-done.19
  473.4 5.2 multiply_reduce_fusion.3
  478.7 1.0 fusion.49
  479.7 8.5 all_gather.7
  488.2 15.3 %fusion.10 = f32[1024,6750]{1,0:T(8,128)} fusion(bf16[256,1024]{1,0:T(8,128)(2,1)S(1)} %all_gather.7, s32[256,6750]{0,1:T(8,128)} %param.17), kind=kOutput, calls=%fused_computation.25 | convolution fusion | flops 3542400000 | bytes 35084288 | tf_op jit(solution)/shard_map/dot_general | solution.py:26
  504.5 0.6 multiply_reduce_fusion.13
  505.1 0.6 add_reduce_fusion
  505.7 1.3 multiply_subtract_fusion
  508.6 41.0 %all-reduce = (f32[]{:T(128)}, f32[1024]{0:T(1024)}, f32[1024]{0:T(1024)}, f32[1024]{0:T(1024)}, f32[1024]{0:T(1024)}, /*index=5*/f32[16,512]{1,0:T(8,128)}, f32[16]{0:T(128)}) all-reduce(f32[]{:T(128)S(6)} %mul.313, f32[1024]{0:T(1024)S(1)} %get-tuple-element.18, ...), channel_id=1, replica_groups=mesh['dp'=16,'gene'=2] {'dp','gene'}, use_global_device_ids=true, to_apply=%region_16.17 | all-reduce | flops 12305 | bytes 98440 | tf_op jit(solution)/shard_map/psum | solution.py:226
  549.6 47.7 %reduce-scatter.41.cloned.1.call-done = f32[64,512]{1,0:T(8,128)} async-done(((f32[1024,512]{1,0:T(8,128)}), f32[64,512]{1,0:T(8,128)}) %reduce-scatter.41.cloned.1.call-update) | async-done | bytes 131088 | tf_op jit(solution)/shard_map/reduce_scatter | solution.py:224
  597.3 147.6 %reduce-scatter.21.cloned.1.call-done = f32[32,6750]{1,0:T(8,128)} async-done(((f32[512,6750]{1,0:T(8,128)}), f32[32,6750]{1,0:T(8,128)}) %reduce-scatter.21.cloned.1.call-update) | async-done | bytes 864016 | tf_op jit(solution)/shard_map/reduce_scatter | solution.py:200
  744.9 88.8 %reduce-scatter.25.cloned.1.call-done = f32[64,1536]{1,0:T(8,128)} async-done(((f32[1024,1536]{1,0:T(8,128)}), f32[64,1536]{1,0:T(8,128)}) %reduce-scatter.25.cloned.1.call-update) | async-done | bytes 393232 | tf_op jit(solution)/shard_map/reduce_scatter | solution.py:220
  833.7 107.1 %reduce-scatter.37.cloned.1.call-done = f32[256,512]{1,0:T(8,128)} async-done(((f32[4096,512]{1,0:T(8,128)}), f32[256,512]{1,0:T(8,128)}) %reduce-scatter.37.cloned.1.call-update) | async-done | bytes 524304 | tf_op jit(solution)/shard_map/reduce_scatter | solution.py:223
  940.9 107.8 %reduce-scatter.33.cloned.1.call-done = f32[64,2048]{1,0:T(8,128)} async-done(((f32[1024,2048]{1,0:T(8,128)}), f32[64,2048]{1,0:T(8,128)}) %reduce-scatter.33.cloned.1.call-update) | async-done | bytes 524304 | tf_op jit(solution)/shard_map/reduce_scatter | solution.py:222
  1048.6 271.7 %reduce-scatter.19.cloned.1.call-done = f32[64,6750]{1,0:T(8,128)} async-done(((f32[1024,6750]{1,0:T(8,128)}), f32[64,6750]{1,0:T(8,128)}) %reduce-scatter.19.cloned.1.call-update) | async-done | bytes 1728016 | tf_op jit(solution)/shard_map/reduce_scatter | solution.py:199
  (187 shorter events, 8.4 us)
Async XLA Ops:
  7.2 48.1 %copy-start = (bf16[1024,1024]{1,0:T(8,128)(2,1)S(1)}, bf16[1024,1024]{1,0:T(8,128)(2,1)}, u32[]{:S(2)}) copy-start(bf16[1024,1024]{1,0:T(8,128)(2,1)} %param.25) | copy-start | bytes 6291460
  7.2 13.0 copy-start.61
  7.2 13.0 copy-start.58
  7.2 35.7 %reduce-scatter.15.cloned.1.call-start = ((), (), s32[]{:S(2)}) async-start(), calls=%async_computation.14 | async-start | bytes 1572864 | tf_op jit(solution)/shard_map/reduce_scatter | solution.py:93
  19.6 25.6 %copy-start.36 = (f32[1024]{0:T(1024)S(1)}, f32[1024]{0:T(1024)}, u32[]{:S(2)}) copy-start(f32[1024]{0:T(1024)} %param.22) | copy-start | bytes 12292
  19.6 25.6 %copy-start.38 = (f32[1024]{0:T(1024)S(1)}, f32[1024]{0:T(1024)}, u32[]{:S(2)}) copy-start(f32[1024]{0:T(1024)} %param.23) | copy-start | bytes 12292
  19.6 78.7 %reduce-scatter.17.cloned.1.call-start = ((), (), s32[]{:S(2)}) async-start(), calls=%async_computation.15 | async-start | bytes 786432 | tf_op jit(solution)/shard_map/reduce_scatter | solution.py:133
  20.3 33.2 %copy-start.48 = (pred[128,128]{0,1:T(8,128)(4,1)}, pred[128,128]{0,1:T(8,128)(4,1)S(1)}, u32[]{:S(2)}) copy-start(pred[128,128]{0,1:T(8,128)(4,1)S(1)} %broadcast_compare_fusion) | copy-start | bytes 49156
  50.0 5.2 copy-start.22
  51.2 4.0 copy-start.24
  53.5 2.3 copy-start.53
  53.5 2.5 copy-start.31
  53.5 2.5 copy-start.35
  55.2 5.7 copy-start.27
  55.8 5.2 copy-start.40
  56.1 4.9 copy-start.43
  56.1 17.8 %slice-start = ((s8[6914048]{0:T(1024)(128)(4,1)}), s8[4194304]{0:T(1024)(128)(4,1)S(1)}, s32[]{:S(2)}) async-start(s8[6914048]{0:T(1024)(128)(4,1)} %bitcast.61), calls=%async_computation.28 | async-start | bytes 8388608
  56.1 17.8 %slice-start.4 = ((s8[6914048]{0:T(1024)(128)(4,1)}), s8[4194304]{0:T(1024)(128)(4,1)S(1)}, s32[]{:S(2)}) async-start(s8[6914048]{0:T(1024)(128)(4,1)} %bitcast.65), calls=%async_computation.32 | async-start | bytes 8388608
  61.0 5.7 copy-start.3
  61.0 5.7 copy-start.6
  61.0 6.1 copy-start.26
  61.0 12.8 slice-start.1
  61.0 12.8 slice-start.5
  73.9 4.0 copy-start.10
  77.8 2.8 copy-start.2
  80.7 2.9 copy-start.59
  80.7 5.4 copy-start.29
  83.5 65.9 %reduce-scatter.27.cloned.1.call-start = ((), (), s32[]{:S(2)}) async-start(), calls=%async_computation.20 | async-start | bytes 3145728 | tf_op jit(solution)/shard_map/reduce_scatter | solution.py:206
  98.3 5.7 copy-start.4
  101.4 9.2 slice-start.2
  104.0 10.3 copy-start.9
  104.0 6.7 slice-start.3
  104.0 6.7 copy-start.41
  104.0 6.7 copy-start.44
  110.7 3.5 copy-start.12
  110.7 4.6 copy-start.28
  117.3 66.1 %reduce-scatter.39.cloned.1.call-start = ((), (), s32[]{:S(2)}) async-start(), calls=%async_computation.26 | async-start | bytes 3145728 | tf_op jit(solution)/shard_map/reduce_scatter | solution.py:215
  120.6 3.9 copy-start.54
  120.6 142.1 %reduce-scatter.23.cloned.1.call-start = ((), (), s32[]{:S(2)}) async-start(), calls=%async_computation.18 | async-start | bytes 9437184 | tf_op jit(solution)/shard_map/reduce_scatter | solution.py:203
  123.3 3.8 copy-start.17
  123.3 3.8 copy-start.34
  127.1 1.4 copy-start.23
  127.1 2.4 copy-start.32
  127.1 2.4 copy-start.37
  127.1 2.4 copy-start.39
  127.1 2.4 copy-start.52
  127.1 2.4 copy-start.57
  134.2 1.6 copy-start.5
  134.2 230.0 %reduce-scatter.35.cloned.1.call-start = ((), (), s32[]{:S(2)}) async-start(), calls=%async_computation.24 | async-start | bytes 12582912 | tf_op jit(solution)/shard_map/reduce_scatter | solution.py:212
  141.5 324.4 %reduce-scatter.31.cloned.1.call-start = ((), (), s32[]{:S(2)}) async-start(), calls=%async_computation.22 | async-start | bytes 12582912 | tf_op jit(solution)/shard_map/reduce_scatter | solution.py:209
  148.4 401.2 %reduce-scatter.29.cloned.1.call-start = ((), (), s32[]{:S(2)}) async-start(), calls=%async_computation.21 | async-start | bytes 2228224 | tf_op jit(solution)/shard_map/reduce_scatter | solution.py:221
  152.2 34.2 %copy-start.11 = (bf16[256,512]{1,0:T(8,128)(2,1)S(1)}, bf16[256,512]{1,0:T(8,128)(2,1)}, u32[]{:S(2)}) copy-start(bf16[256,512]{1,0:T(8,128)(2,1)} %copy-done.10) | copy-start | bytes 786436
  152.2 445.1 %reduce-scatter.41.cloned.1.call-start = ((), (), s32[]{:S(2)}) async-start(), calls=%async_computation.27 | async-start | bytes 2228224 | tf_op jit(solution)/shard_map/reduce_scatter | solution.py:224
  186.3 558.6 %reduce-scatter.21.cloned.1.call-start = ((), (), s32[]{:S(2)}) async-start(), calls=%async_computation.17 | async-start | bytes 14761984 | tf_op jit(solution)/shard_map/reduce_scatter | solution.py:200
  196.6 637.2 %reduce-scatter.25.cloned.1.call-start = ((), (), s32[]{:S(2)}) async-start(), calls=%async_computation.19 | async-start | bytes 6684672 | tf_op jit(solution)/shard_map/reduce_scatter | solution.py:220
  268.2 672.6 %reduce-scatter.37.cloned.1.call-start = ((), (), s32[]{:S(2)}) async-start(), calls=%async_computation.25 | async-start | bytes 8912896 | tf_op jit(solution)/shard_map/reduce_scatter | solution.py:223
  370.9 677.7 %reduce-scatter.33.cloned.1.call-start = ((), (), s32[]{:S(2)}) async-start(), calls=%async_computation.23 | async-start | bytes 8912896 | tf_op jit(solution)/shard_map/reduce_scatter | solution.py:222
  472.4 6.3 copy-start.8
  472.4 847.9 %reduce-scatter.19.cloned.1.call-start = ((), (), s32[]{:S(2)}) async-start(), calls=%async_computation.16 | async-start | bytes 29523968 | tf_op jit(solution)/shard_map/reduce_scatter | solution.py:199
  503.5 2.2 copy-start.60
  503.5 3.5 copy-start.30
  503.5 5.1 copy-start.46
  503.5 5.1 copy-start.47
  503.6 816.7 %copy-start.1 = (bf16[1024,1024]{1,0:T(8,128)(2,1)S(1)}, bf16[1024,1024]{1,0:T(8,128)(2,1)}, u32[]{:S(2)}) copy-start(bf16[1024,1024]{1,0:T(8,128)(2,1)} %param.25) | copy-start | bytes 6291460
  (18 other events, 15.5 us)
Sparse Core Ops, SparseCore 0:
  19.7 23.1 reduce-scatter.14
  83.6 14.6 reduce-scatter.16
  117.4 31.9 reduce-scatter.26
  151.5 31.8 reduce-scatter.38
  185.6 77.1 reduce-scatter.22
  264.9 99.3 reduce-scatter.34
  366.5 99.3 reduce-scatter.30
  470.2 61.8 reduce-scatter.28
  536.4 60.8 reduce-scatter.40
  601.9 143.0 reduce-scatter.20
  749.5 84.2 reduce-scatter.24
  838.2 102.5 reduce-scatter.36
  945.5 103.0 reduce-scatter.32
  1053.2 267.0 reduce-scatter.18
where the time goes:
time: 1330 us
  waiting for transfers between devices  1090 us (82%)
  matrix products  111 us (8%)
  blocking collectives  55.3 us (4%)
  other arithmetic  34.4 us (3%)
  between operations  18 us (1%)
  local copies, waits for them, and re-layouts  15 us (1%)
    reduce_scatter x1, waiting for transfers between devices, shards(): lax.psum_scatter(grad_table_local, 'dp', scatter_dimension=0, tiled=True)  272 us
    reduce_scatter x1, waiting for transfers between devices, shards(): lax.psum_scatter(grad_dec_local, 'dp', scatter_dimension=0, tiled=True)  148 us
    reduce_scatter x1, waiting for transfers between devices, shards(): lax.psum_scatter(gene_up, 'dp', scatter_dimension=0, tiled=True)  108 us
    reduce_scatter x1, waiting for transfers between devices, shards(): lax.psum_scatter(gene_down, 'dp', scatter_dimension=0, tiled=True)  107 us
    reduce_scatter x1, waiting for transfers between devices, shards(): lax.psum_scatter(grad_w_down.astype(jnp.bfloat16), 'gene', scatter_dimens...  95.7 us
    reduce_scatter x1, waiting for transfers between devices, shards(): lax.psum_scatter(grad_w_up.astype(jnp.bfloat16), 'gene', scatter_dimensio...  95 us
    reduce_scatter x1, waiting for transfers between devices, shards(): lax.psum_scatter(gene_qkv, 'dp', scatter_dimension=0, tiled=True)  88.8 us
    reduce_scatter x1, waiting for transfers between devices, shards(): lax.psum_scatter(grad_w_qkv.astype(jnp.bfloat16), 'gene', scatter_dimensi...  66.1 us
  transfers between devices with their start and end apart: 14, of which 13 were waited for; matrix products, arithmetic and copies ran while one was open for 7% of the time, Pallas kernels for 0%

commit v1 on v0

--- a/solution.py
+++ b/solution.py
@@ -196,32 +196,46 @@
         lax.all_gather(grad_embed_low, "gene", axis=0, tiled=True), expr_low
     )
     table_part, decode_part = (
-        lax.psum_scatter(grad_table_local, "dp", scatter_dimension=0, tiled=True),
-        lax.psum_scatter(grad_dec_local, "dp", scatter_dimension=0, tiled=True),
+        lax.psum_scatter(
+            grad_table_local.astype(jnp.bfloat16), "dp", scatter_dimension=0, tiled=True
+        ).astype(jnp.float32),
+        lax.psum_scatter(
+            grad_dec_local.astype(jnp.bfloat16), "dp", scatter_dimension=0, tiled=True
+        ).astype(jnp.float32),
     )
     gene_qkv, gene_out, gene_up, gene_down, gene_latent = (
         lax.psum_scatter(
             grad_w_qkv.astype(jnp.bfloat16), "gene", scatter_dimension=1, tiled=True
-        ).astype(jnp.float32),
+        ),
         lax.psum_scatter(
             grad_w_out.astype(jnp.bfloat16), "gene", scatter_dimension=1, tiled=True
-        ).astype(jnp.float32),
+        ),
         lax.psum_scatter(
             grad_w_up.astype(jnp.bfloat16), "gene", scatter_dimension=1, tiled=True
-        ).astype(jnp.float32),
+        ),
         lax.psum_scatter(
             grad_w_down.astype(jnp.bfloat16), "gene", scatter_dimension=1, tiled=True
-        ).astype(jnp.float32),
+        ),
         lax.psum_scatter(
             grad_w_latent.astype(jnp.bfloat16), "gene", scatter_dimension=1, tiled=True
-        ).astype(jnp.float32),
+        ),
     )
     sum_qkv, sum_out, sum_up, sum_down, sum_latent = (
-        lax.psum_scatter(gene_qkv, "dp", scatter_dimension=0, tiled=True),
-        lax.psum_scatter(gene_out, "dp", scatter_dimension=0, tiled=True),
-        lax.psum_scatter(gene_up, "dp", scatter_dimension=0, tiled=True),
-        lax.psum_scatter(gene_down, "dp", scatter_dimension=0, tiled=True),
-        lax.psum_scatter(gene_latent, "dp", scatter_dimension=0, tiled=True),
+        lax.psum_scatter(gene_qkv, "dp", scatter_dimension=0, tiled=True).astype(
+            jnp.float32
+        ),
+        lax.psum_scatter(gene_out, "dp", scatter_dimension=0, tiled=True).astype(
+            jnp.float32
+        ),
+        lax.psum_scatter(gene_up, "dp", scatter_dimension=0, tiled=True).astype(
+            jnp.float32
+        ),
+        lax.psum_scatter(gene_down, "dp", scatter_dimension=0, tiled=True).astype(
+            jnp.float32
+        ),
+        lax.psum_scatter(gene_latent, "dp", scatter_dimension=0, tiled=True).astype(
+            jnp.float32
+        ),
     )
     loss_total, logits_total, means_total, sum_gain1, sum_bias1, sum_gain2, sum_bias2 = lax.psum(
         (

time: 1330 us -> 1070 us (0.80)
  waiting for transfers between devices: 1090 us -> 838 us
    reduce_scatter x2, waiting for transfers between devices: 419 us -> 236 us  [the longest x1 145 us: shards(): lax.psum_scatter(grad_table_local.astype(jnp.bfloat16), 'dp', scatter_dim...]
    reduce_scatter x1, waiting for transfers between devices: 108 us -> 73.8 us  [shards(): lax.psum_scatter(gene_up, 'dp', scatter_dimension=0, tiled=True)]
    reduce_scatter x1, waiting for transfers between devices: 107 us -> 73.4 us  [shards(): lax.psum_scatter(gene_down, 'dp', scatter_dimension=0, tiled=True)]
    reduce_scatter x1, waiting for transfers between devices: 95.7 us -> 72.7 us  [shards(): lax.psum_scatter(grad_w_down.astype(jnp.bfloat16), 'gene', scatter_dimens...]
    reduce_scatter x1, waiting for transfers between devices: 88.8 us -> 67.8 us  [shards(): lax.psum_scatter(gene_qkv, 'dp', scatter_dimension=0, tiled=True)]
    reduce_scatter x1, waiting for transfers between devices: 0.01 us -> 15.4 us  [shards(): lax.psum_scatter(gene_out, 'dp', scatter_dimension=0, tiled=True)]
  transfers between devices with their start and end apart: 14 -> 14, of which waited for: 13 -> 14; matrix products, arithmetic and copies ran while one was open for 7% -> 7% of each run, Pallas kernels for 0% -> 0%
where the time goes in v1:
time: 1070 us; the launch traced here: 1060 us
  waiting for transfers between devices  838 us (78%)
  matrix products  106 us (10%)
  blocking collectives  61 us (6%)
  other arithmetic  22.9 us (2%)
  between operations  17.8 us (2%)
  local copies, waits for them, and re-layouts  13.9 us (1%)
    reduce_scatter x1, waiting for transfers between devices, shards(): lax.psum_scatter(grad_table_local.astype(jnp.bfloat16), 'dp', scatter_dim...  145 us
    reduce_scatter x1, waiting for transfers between devices, shards(): lax.psum_scatter(grad_w_up.astype(jnp.bfloat16), 'gene', scatter_dimensio...  102 us
    reduce_scatter x1, waiting for transfers between devices, shards(): lax.psum_scatter(grad_dec_local.astype(jnp.bfloat16), 'dp', scatter_dimen...  90.7 us
    reduce_scatter x1, waiting for transfers between devices, shards(): lax.psum_scatter(gene_up, 'dp', scatter_dimension=0, tiled=True)  73.8 us
    reduce_scatter x1, waiting for transfers between devices, shards(): lax.psum_scatter(gene_down, 'dp', scatter_dimension=0, tiled=True)  73.4 us
    reduce_scatter x1, waiting for transfers between devices, shards(): lax.psum_scatter(grad_w_down.astype(jnp.bfloat16), 'gene', scatter_dimens...  72.7 us
    reduce_scatter x1, waiting for transfers between devices, shards(): lax.psum_scatter(grad_w_qkv.astype(jnp.bfloat16), 'gene', scatter_dimensi...  71.2 us
    reduce_scatter x1, waiting for transfers between devices, shards(): lax.psum_scatter(gene_qkv, 'dp', scatter_dimension=0, tiled=True)  67.8 us
  transfers between devices with their start and end apart: 14, of which 14 were waited for; matrix products, arithmetic and copies ran while one was open for 7% of the time, Pallas kernels for 0%

profile of v1, /device:TPU:0, one launch (start us, length us, event | category | flops | bytes accessed | tf_op | source)
XLA Modules:
  0.0 1061.5 jit_solution(17172421481558509745)
XLA Ops:
  7.3 12.3 %fusion.11 = f32[256,1024]{1,0:T(8,128)} fusion(bf16[6750,1024]{1,0:T(8,128)(2,1)} %param.21, s32[256,6750]{0,1:T(8,128)} %param.17), kind=kOutput, calls=%fused_computation.27 | convolution fusion | flops 3542400000 | bytes 21784576 | tf_op jit(solution)/shard_map/dot_general | solution.py:22
  20.3 1.0 multiply_sine_fusion.1
  21.3 21.6 %reduce-scatter.15.cloned.1.call-done = f32[128,1024]{1,0:T(8,128)} async-done(((f32[256,1024]{1,0:T(8,128)}), f32[128,1024]{1,0:T(8,128)}) %reduce-scatter.15.cloned.1.call-update) | async-done | bytes 524304 | tf_op jit(solution)/shard_map/reduce_scatter | solution.py:93
  42.9 1.2 fusion.48
  45.1 3.8 convolution_convert_fusion.5
  49.0 0.8 fusion.49
  49.9 1.2 copy.46
  51.1 0.8 copy.45
  52.0 1.5 fusion.50
  53.5 1.7 convolution_convert_fusion.10
  56.0 4.9 fusion.46
  61.0 5.6 fusion.14
  67.9 5.9 all_gather.6
  73.8 4.0 multiply_reduce_fusion
  77.8 2.8 copy-done.2
  80.6 2.8 fusion.13
  83.5 0.6 reduce_max.29
  84.1 1.2 exponential_reduce_fusion
  86.2 0.7 subtract_subtract_fusion
  87.7 10.5 reduce-scatter.17.cloned.1.call-done
  98.2 2.5 add_convert_fusion.2
  100.7 0.7 copy-done.16
  101.4 2.6 fusion.27
  104.0 6.6 fusion.2
  110.7 3.5 multiply_reduce_fusion.2
  114.5 0.8 copy-done.7
  115.3 2.0 convolution_convert_fusion.7
  117.5 3.0 convolution_convert_fusion.6
  120.6 2.6 convolution_convert_fusion.9
  123.2 1.3 copy.49
  124.5 2.5 convolution_convert_fusion.8
  129.5 4.6 convolution_convert_fusion.4
  134.1 1.5 copy-done.5
  135.7 5.6 convolution_convert_fusion.2
  141.4 1.1 copy-done.13
  142.5 5.8 convolution_convert_fusion.3
  148.4 0.9 reduce-scatter.27.cloned.1.call-done
  149.4 34.0 %reduce-scatter.39.cloned.1.call-done = bf16[1024,512]{1,0:T(8,128)(2,1)} async-done(((bf16[1024,1024]{1,0:T(8,128)(2,1)}), bf16[1024,512]{1,0:T(8,128)(2,1)}) %reduce-scatter.39.cloned.1.call-update) | async-done | bytes 1048592 | tf_op jit(solution)/shard_map/reduce_scatter | solution.py:219
  183.5 7.9 convolution_convert_fusion.1
  191.5 71.2 %reduce-scatter.23.cloned.1.call-done = bf16[1024,1536]{1,0:T(8,128)(2,1)} async-done(((bf16[1024,3072]{1,0:T(8,128)(2,1)}), bf16[1024,1536]{1,0:T(8,128)(2,1)}) %reduce-scatter.23.cloned.1.call-update) | async-done | bytes 3145744 | tf_op jit(solution)/shard_map/reduce_scatter | solution.py:207
  263.1 5.1 multiply_reduce_fusion.3
  268.2 1.0 fusion.47
  269.3 14.3 %all_gather.7 = bf16[256,1024]{1,0:T(8,128)(2,1)S(1)} all-gather(bf16[128,1024]{1,0:T(8,128)(2,1)S(1)} %get-tuple-element.31), channel_id=1, replica_groups=mesh['dp'=16,'gene'=2] {'gene'}, dimensions={0}, use_global_device_ids=true | all-gather | bytes 786432 | tf_op jit(solution)/shard_map/all_gather | solution.py:196
  283.6 12.8 %convolution_convert_fusion = bf16[1024,6750]{1,0:T(8,128)(2,1)} fusion(bf16[256,1024]{1,0:T(8,128)(2,1)S(1)} %all_gather.7, s32[256,6750]{0,1:T(8,128)} %param.17), kind=kOutput, calls=%fused_computation.1 | convolution fusion | flops 3549312000 | bytes 21260288 | tf_op jit(solution)/shard_map/dot_general | solution.py:26
  296.5 72.7 %reduce-scatter.35.cloned.1.call-done = bf16[4096,512]{1,0:T(8,128)(2,1)} async-done(((bf16[4096,1024]{1,0:T(8,128)(2,1)}), bf16[4096,512]{1,0:T(8,128)(2,1)}) %reduce-scatter.35.cloned.1.call-update) | async-done | bytes 4194320 | tf_op jit(solution)/shard_map/reduce_scatter | solution.py:216
  369.3 101.6 %reduce-scatter.31.cloned.1.call-done = bf16[1024,2048]{1,0:T(8,128)(2,1)} async-done(((bf16[1024,4096]{1,0:T(8,128)(2,1)}), bf16[1024,2048]{1,0:T(8,128)(2,1)}) %reduce-scatter.31.cloned.1.call-update) | async-done | bytes 4194320 | tf_op jit(solution)/shard_map/reduce_scatter | solution.py:213
  471.9 0.6 multiply_reduce_fusion.13
  472.5 0.6 add_reduce_fusion
  473.1 1.3 multiply_subtract_fusion
  476.0 40.7 %all-reduce = (f32[]{:T(128)}, f32[1024]{0:T(1024)}, f32[1024]{0:T(1024)}, f32[1024]{0:T(1024)}, f32[1024]{0:T(1024)}, /*index=5*/f32[16,512]{1,0:T(8,128)}, f32[16]{0:T(128)}) all-reduce(f32[]{:T(128)S(6)} %mul.313, f32[1024]{0:T(1024)S(1)} %get-tuple-element.18, ...), channel_id=1, replica_groups=mesh['dp'=16,'gene'=2] {'dp','gene'}, use_global_device_ids=true, to_apply=%region_16.17 | all-reduce | flops 12305 | bytes 98440 | tf_op jit(solution)/shard_map/psum | solution.py:240
  516.7 15.4 %reduce-scatter.29.cloned.1.call-done = bf16[64,512]{1,0:T(8,128)(2,1)} async-done(((bf16[1024,512]{1,0:T(8,128)(2,1)}), bf16[64,512]{1,0:T(8,128)(2,1)}) %reduce-scatter.29.cloned.1.call-update) | async-done | bytes 65552 | tf_op jit(solution)/shard_map/reduce_scatter | solution.py:227
  532.2 1.5 convert_element_type.128
  533.7 58.8 %reduce-scatter.41.cloned.1.call-done = bf16[64,512]{1,0:T(8,128)(2,1)} async-done(((bf16[1024,512]{1,0:T(8,128)(2,1)}), bf16[64,512]{1,0:T(8,128)(2,1)}) %reduce-scatter.41.cloned.1.call-update) | async-done | bytes 65552 | tf_op jit(solution)/shard_map/reduce_scatter | solution.py:236
  592.5 1.5 convert_element_type.134
  594.0 90.7 %reduce-scatter.21.cloned.1.call-done = bf16[32,6750]{1,0:T(8,128)(2,1)} async-done(((bf16[512,6750]{1,0:T(8,128)(2,1)}), bf16[32,6750]{1,0:T(8,128)(2,1)}) %reduce-scatter.21.cloned.1.call-update) | async-done | bytes 432016 | tf_op jit(solution)/shard_map/reduce_scatter | solution.py:202
  684.6 2.0 convert_element_type.124
  686.6 67.8 %reduce-scatter.25.cloned.1.call-done = bf16[64,1536]{1,0:T(8,128)(2,1)} async-done(((bf16[1024,1536]{1,0:T(8,128)(2,1)}), bf16[64,1536]{1,0:T(8,128)(2,1)}) %reduce-scatter.25.cloned.1.call-update) | async-done | bytes 196624 | tf_op jit(solution)/shard_map/reduce_scatter | solution.py:224
  754.4 1.7 convert_element_type.126
  756.1 145.3 %reduce-scatter.19.cloned.1.call-done = bf16[64,6750]{1,0:T(8,128)(2,1)} async-done(((bf16[1024,6750]{1,0:T(8,128)(2,1)}), bf16[64,6750]{1,0:T(8,128)(2,1)}) %reduce-scatter.19.cloned.1.call-update) | async-done | bytes 864016 | tf_op jit(solution)/shard_map/reduce_scatter | solution.py:199
  901.4 2.5 convert_element_type.122
  903.9 73.4 %reduce-scatter.37.cloned.1.call-done = bf16[256,512]{1,0:T(8,128)(2,1)} async-done(((bf16[4096,512]{1,0:T(8,128)(2,1)}), bf16[256,512]{1,0:T(8,128)(2,1)}) %reduce-scatter.37.cloned.1.call-update) | async-done | bytes 262160 | tf_op jit(solution)/shard_map/reduce_scatter | solution.py:233
  977.3 1.8 convert_element_type.132
  979.1 73.8 %reduce-scatter.33.cloned.1.call-done = bf16[64,2048]{1,0:T(8,128)(2,1)} async-done(((bf16[1024,2048]{1,0:T(8,128)(2,1)}), bf16[64,2048]{1,0:T(8,128)(2,1)}) %reduce-scatter.33.cloned.1.call-update) | async-done | bytes 262160 | tf_op jit(solution)/shard_map/reduce_scatter | solution.py:230
  1052.9 1.8 convert_element_type.130
  (189 shorter events, 9.3 us)
Async XLA Ops:
  7.2 48.0 %copy-start = (bf16[1024,1024]{1,0:T(8,128)(2,1)S(1)}, bf16[1024,1024]{1,0:T(8,128)(2,1)}, u32[]{:S(2)}) copy-start(bf16[1024,1024]{1,0:T(8,128)(2,1)} %param.25) | copy-start | bytes 6291460
  7.2 13.0 %copy-start.61 = (f32[128,2]{0,1:T(2,128)S(1)}, f32[128,2]{0,1:T(2,128)}, u32[]{:S(2)}) copy-start(f32[128,2]{0,1:T(2,128)} %param.18) | copy-start | bytes 3076
  7.2 13.0 %copy-start.58 = (s32[1,128]{1,0:T(1,128)S(1)}, s32[1,128]{1,0:T(1,128)}, u32[]{:S(2)}) copy-start(s32[1,128]{1,0:T(1,128)} %param.19) | copy-start | bytes 1540
  7.2 35.7 %reduce-scatter.15.cloned.1.call-start = ((), (), s32[]{:S(2)}) async-start(), calls=%async_computation.14 | async-start | bytes 1572864 | tf_op jit(solution)/shard_map/reduce_scatter | solution.py:93
  19.6 25.5 %copy-start.36 = (f32[1024]{0:T(1024)S(1)}, f32[1024]{0:T(1024)}, u32[]{:S(2)}) copy-start(f32[1024]{0:T(1024)} %param.22) | copy-start | bytes 12292
  19.6 25.5 %copy-start.38 = (f32[1024]{0:T(1024)S(1)}, f32[1024]{0:T(1024)}, u32[]{:S(2)}) copy-start(f32[1024]{0:T(1024)} %param.23) | copy-start | bytes 12292
  19.6 78.6 %reduce-scatter.17.cloned.1.call-start = ((), (), s32[]{:S(2)}) async-start(), calls=%async_computation.15 | async-start | bytes 786432 | tf_op jit(solution)/shard_map/reduce_scatter | solution.py:133
  20.3 33.1 %copy-start.48 = (pred[128,128]{0,1:T(8,128)(4,1)}, pred[128,128]{0,1:T(8,128)(4,1)S(1)}, u32[]{:S(2)}) copy-start(pred[128,128]{0,1:T(8,128)(4,1)S(1)} %broadcast_compare_fusion) | copy-start | bytes 49156
  49.9 5.2 copy-start.22
  51.1 4.0 copy-start.24
  53.5 2.5 copy-start.31
  53.5 2.5 copy-start.35
  55.2 5.7 copy-start.27
  55.7 5.2 copy-start.40
  56.0 4.9 copy-start.43
  56.0 17.8 %slice-start = ((s8[6914048]{0:T(1024)(128)(4,1)}), s8[4194304]{0:T(1024)(128)(4,1)S(1)}, s32[]{:S(2)}) async-start(s8[6914048]{0:T(1024)(128)(4,1)} %bitcast.61), calls=%async_computation.28 | async-start | bytes 8388608
  56.0 17.8 %slice-start.4 = ((s8[6914048]{0:T(1024)(128)(4,1)}), s8[4194304]{0:T(1024)(128)(4,1)S(1)}, s32[]{:S(2)}) async-start(s8[6914048]{0:T(1024)(128)(4,1)} %bitcast.65), calls=%async_computation.32 | async-start | bytes 8388608
  60.9 5.7 copy-start.3
  60.9 5.7 copy-start.6
  60.9 6.1 copy-start.26
  61.0 12.8 %slice-start.1 = ((s8[6914048]{0:T(1024)(128)(4,1)}), s8[2719744]{0:T(1024)(128)(4,1)S(1)}, s32[]{:S(2)}) async-start(s8[6914048]{0:T(1024)(128)(4,1)} %bitcast.61), calls=%async_computation.29 | async-start | bytes 5439488
  61.0 12.8 %slice-start.5 = ((s8[6914048]{0:T(1024)(128)(4,1)}), s8[2719744]{0:T(1024)(128)(4,1)S(1)}, s32[]{:S(2)}) async-start(s8[6914048]{0:T(1024)(128)(4,1)} %bitcast.65), calls=%async_computation.33 | async-start | bytes 5439488
  73.8 4.0 copy-start.9
  77.8 2.8 copy-start.2
  80.6 2.9 copy-start.59
  80.6 5.4 copy-start.29
  83.4 65.9 %reduce-scatter.27.cloned.1.call-start = ((), (), s32[]{:S(2)}) async-start(), calls=%async_computation.20 | async-start | bytes 3145728 | tf_op jit(solution)/shard_map/reduce_scatter | solution.py:210
  98.2 5.7 copy-start.4
  101.4 9.2 slice-start.2
  103.9 10.3 copy-start.11
  103.9 6.7 slice-start.3
  104.0 6.7 copy-start.41
  104.0 6.7 copy-start.44
  110.6 3.6 copy-start.12
  110.7 4.6 copy-start.28
  117.3 66.1 %reduce-scatter.39.cloned.1.call-start = ((), (), s32[]{:S(2)}) async-start(), calls=%async_computation.26 | async-start | bytes 3145728 | tf_op jit(solution)/shard_map/reduce_scatter | solution.py:219
  120.6 3.9 copy-start.54
  120.6 142.1 %reduce-scatter.23.cloned.1.call-start = ((), (), s32[]{:S(2)}) async-start(), calls=%async_computation.18 | async-start | bytes 9437184 | tf_op jit(solution)/shard_map/reduce_scatter | solution.py:207
  123.2 3.8 copy-start.17
  123.2 3.8 copy-start.34
  127.0 2.4 copy-start.32
  127.1 2.4 copy-start.37
  127.1 2.4 copy-start.39
  134.1 235.1 %reduce-scatter.35.cloned.1.call-start = ((), (), s32[]{:S(2)}) async-start(), calls=%async_computation.24 | async-start | bytes 12582912 | tf_op jit(solution)/shard_map/reduce_scatter | solution.py:216
  141.3 329.5 %reduce-scatter.31.cloned.1.call-start = ((), (), s32[]{:S(2)}) async-start(), calls=%async_computation.22 | async-start | bytes 12582912 | tf_op jit(solution)/shard_map/reduce_scatter | solution.py:213
  148.4 35.1 %copy-start.10 = (bf16[256,512]{1,0:T(8,128)(2,1)S(1)}, bf16[256,512]{1,0:T(8,128)(2,1)}, u32[]{:S(2)}) copy-start(bf16[256,512]{1,0:T(8,128)(2,1)} %copy-done.9) | copy-start | bytes 786436
  148.4 383.8 %reduce-scatter.29.cloned.1.call-start = ((), (), s32[]{:S(2)}) async-start(), calls=%async_computation.21 | async-start | bytes 1114112 | tf_op jit(solution)/shard_map/reduce_scatter | solution.py:227
  149.4 443.1 %reduce-scatter.41.cloned.1.call-start = ((), (), s32[]{:S(2)}) async-start(), calls=%async_computation.27 | async-start | bytes 1114112 | tf_op jit(solution)/shard_map/reduce_scatter | solution.py:236
  183.4 501.2 %reduce-scatter.21.cloned.1.call-start = ((), (), s32[]{:S(2)}) async-start(), calls=%async_computation.17 | async-start | bytes 7380992 | tf_op jit(solution)/shard_map/reduce_scatter | solution.py:202
  191.4 71.6 %copy-start.19 = (bf16[16,64,128]{2,1,0:T(8,128)(2,1)S(1)}, bf16[16,64,128]{2,1,0:T(8,128)(2,1)}, u32[]{:S(2)}) copy-start(bf16[16,64,128]{2,1,0:T(8,128)(2,1)} %copy-done.18) | copy-start | bytes 786436
  191.4 71.6 %copy-start.21 = (bf16[16,64,128]{2,1,0:T(8,128)(2,1)S(1)}, bf16[16,64,128]{2,1,0:T(8,128)(2,1)}, u32[]{:S(2)}) copy-start(bf16[16,64,128]{2,1,0:T(8,128)(2,1)} %copy-done.20) | copy-start | bytes 786436
  191.4 71.6 %copy-start.33 = (bf16[16,64,128]{2,1,0:T(8,128)(2,1)S(1)}, bf16[16,64,128]{2,1,0:T(8,128)(2,1)}, u32[]{:S(2)}) copy-start(bf16[16,64,128]{2,1,0:T(8,128)(2,1)} %convolution_convert_fusion.8) | copy-start | bytes 786436
  191.4 563.0 %reduce-scatter.25.cloned.1.call-start = ((), (), s32[]{:S(2)}) async-start(), calls=%async_computation.19 | async-start | bytes 3342336 | tf_op jit(solution)/shard_map/reduce_scatter | solution.py:224
  262.7 5.5 copy-start.8
  262.7 638.7 %reduce-scatter.19.cloned.1.call-start = ((), (), s32[]{:S(2)}) async-start(), calls=%async_computation.16 | async-start | bytes 14761984 | tf_op jit(solution)/shard_map/reduce_scatter | solution.py:199
  296.5 680.8 %reduce-scatter.37.cloned.1.call-start = ((), (), s32[]{:S(2)}) async-start(), calls=%async_computation.25 | async-start | bytes 4456448 | tf_op jit(solution)/shard_map/reduce_scatter | solution.py:233
  369.2 102.5 %copy-start.50 = (f32[128]{0:T(128)S(1)}, f32[128]{0:T(128)}, u32[]{:S(2)}) copy-start(f32[128]{0:T(128)} %copy-done.49) | copy-start | bytes 1540
  369.2 102.5 %copy-start.55 = (f32[128]{0:T(128)S(1)}, f32[128]{0:T(128)}, u32[]{:S(2)}) copy-start(f32[128]{0:T(128)} %fusion.33) | copy-start | bytes 1540
  369.2 103.8 %copy-start.60 = (f32[16]{0:T(128)S(1)}, f32[16]{0:T(128)}, u32[]{:S(2)}) copy-start(f32[16]{0:T(128)} %param.32) | copy-start | bytes 196
  369.2 105.1 %copy-start.30 = (f32[16,512]{1,0:T(8,128)S(1)}, f32[16,512]{1,0:T(8,128)}, u32[]{:S(2)}) copy-start(f32[16,512]{1,0:T(8,128)} %param.31) | copy-start | bytes 98308
  369.2 106.7 %copy-start.46 = (f32[1024]{0:T(1024)S(1)}, f32[1024]{0:T(1024)}, u32[]{:S(2)}) copy-start(f32[1024]{0:T(1024)} %get-tuple-element.16) | copy-start | bytes 12292
  369.2 106.7 %copy-start.47 = (f32[1024]{0:T(1024)S(1)}, f32[1024]{0:T(1024)}, u32[]{:S(2)}) copy-start(f32[1024]{0:T(1024)} %get-tuple-element.22) | copy-start | bytes 12292
  369.3 683.6 %reduce-scatter.33.cloned.1.call-start = ((), (), s32[]{:S(2)}) async-start(), calls=%async_computation.23 | async-start | bytes 4456448 | tf_op jit(solution)/shard_map/reduce_scatter | solution.py:230
  470.9 583.8 %copy-start.1 = (bf16[1024,1024]{1,0:T(8,128)(2,1)S(1)}, bf16[1024,1024]{1,0:T(8,128)(2,1)}, u32[]{:S(2)}) copy-start(bf16[1024,1024]{1,0:T(8,128)(2,1)} %param.25) | copy-start | bytes 6291460
  (18 other events, 20.6 us)
Sparse Core Ops, SparseCore 0:
  19.7 23.1 reduce-scatter.14
  83.6 14.6 reduce-scatter.16
  117.4 31.9 reduce-scatter.26
  151.5 31.8 reduce-scatter.38
  185.6 77.1 reduce-scatter.22
  264.9 104.3 reduce-scatter.34
  371.5 99.3 reduce-scatter.30
  474.5 57.6 reduce-scatter.28
  535.8 56.6 reduce-scatter.40
  596.3 88.2 reduce-scatter.20
  688.4 65.9 reduce-scatter.24
  758.4 143.0 reduce-scatter.18
  905.3 71.9 reduce-scatter.36
  981.0 71.8 reduce-scatter.32
